TPU v7x, 32 devices: a whole 2x2x4 slice. The times are simulated.
32 devices in a mesh: shot: 8 (over z, y), grp: 4 (over x, core).
Axes of the slice: x: 2, y: 2, z: 4, core: 2. Of those that a mesh axis runs over, the one named last changes fastest.
Arguments:
- offsets: bfloat16 [6144, 32, 512], P(('shot', 'grp')), may hold values from -500 to 500
- slant_weights: bfloat16 [64, 32], replicated, may hold values from -1 to 1
- live: int32 [6144, 64], P(('shot', 'grp')), may hold values from 0 to 1, as said below
- block_tile: int32 [3072, 1], P(('shot', 'grp')), may hold values from 0 to 7; in each aligned block of 96 rows (0 to 95, 96 to 191, ...) at most 13 rows name the same one
- image_slot: int32 [3072], P(('shot', 'grp')), may hold values from 0 to 15
Outputs:
- image: bfloat16 [128, 128, 512], P(('shot', 'grp'))
Inputs may be any that keep to these rules, and one draw needn't show every extreme that they name: Each position's live angles are 0 up to a cutoff minus 1, the cutoff at least 16; the first position of every 192 positions keeps all 64 angles. `block_tile`: among the 96 blocks of one device no tile is named more than 13 times.
All inputs are finite; a program needn't handle non-finite values.
Results may differ from a plain program's by a relative error of at most 0.0049.
Values may be sent and summed in bfloat16 or wider, within the bound.
A program may use at most 192 MiB of HBM per device.

v0:
```python
import jax
import jax.numpy as jnp
from jax import lax
from jax.sharding import PartitionSpec as P

IMG_DEV = 4


def slant_stack(gathers, weights, live_mask):
    slanted = jnp.einsum("ah,phz->paz", weights, gathers, preferred_element_type=jnp.float32)
    return (slanted * live_mask[:, :, None]).astype(jnp.bfloat16)


def angle_moments(angles, live_mask):
    widened = angles.astype(jnp.float32)
    return (jnp.sum(widened * widened, axis=(0, 2)), jnp.sum(live_mask, axis=0))


def global_gain(square_sum, live_count, depth_len):
    totals = lax.psum((square_sum, live_count), ("shot", "grp"))
    return lax.rsqrt(totals[0] / (depth_len * totals[1]) + 1e-06)


def local(offsets, slant_weights, live, block_tile, image_slot):
    peer_count = lax.axis_size("shot")
    block_count = block_tile.shape[0]
    capacity = block_count // peer_count + 1
    slot_count = peer_count * capacity
    depth_len = offsets.shape[2]
    angle_count = slant_weights.shape[0]
    traces = 2 * angle_count
    tile_ids = block_tile[:, 0]
    block_index = jnp.arange(block_count)
    earlier = (tile_ids[:, None] == tile_ids[None, :]) & (
        block_index[None, :] < block_index[:, None]
    )
    slot_rank = jnp.sum(earlier.astype(jnp.int32), axis=1)
    targets = tile_ids * capacity + slot_rank
    labels = (
        jnp.full((slot_count,), -1.0, jnp.float32).at[targets].set(image_slot.astype(jnp.float32))
    )
    labels = labels.astype(jnp.bfloat16).reshape(peer_count, capacity)
    inner = offsets.shape[1:]
    raw_sent = (
        jnp.zeros((slot_count, 2) + inner, jnp.bfloat16)
        .at[targets]
        .set(offsets.reshape((block_count, 2) + inner))
    )
    live_sent = (
        jnp.zeros((slot_count, traces), jnp.bfloat16)
        .at[targets]
        .set(live.reshape(block_count, traces).astype(jnp.bfloat16))
    )
    raw_in, live_in, labels_in = (
        lax.all_to_all(
            raw_sent.reshape((peer_count, capacity, 2) + inner),
            "shot",
            split_axis=0,
            concat_axis=0,
            tiled=True,
        ),
        lax.all_to_all(
            live_sent.reshape(peer_count, capacity, traces),
            "shot",
            split_axis=0,
            concat_axis=0,
            tiled=True,
        ),
        lax.all_to_all(labels, "shot", split_axis=0, concat_axis=0, tiled=True),
    )
    mask_in = live_in.reshape(slot_count * 2, angle_count).astype(jnp.float32)
    angles = slant_stack(raw_in.reshape((slot_count * 2,) + inner), slant_weights, mask_in)
    square_sum, live_count = angle_moments(angles, mask_in)
    received = angles.reshape(slot_count, traces * depth_len)
    angle_gain = global_gain(square_sum, live_count, depth_len)
    tile_rows = IMG_DEV * lax.axis_size("grp")
    slot_codes = labels_in.reshape(slot_count).astype(jnp.float32)
    holder = (slot_codes[None, :] == jnp.arange(tile_rows, dtype=jnp.float32)[:, None]).astype(
        jnp.bfloat16
    )
    stacked = lax.psum_scatter(
        jnp.dot(holder, received, preferred_element_type=jnp.float32),
        "grp",
        scatter_dimension=0,
        tiled=True,
    )
    trace_gain = jnp.tile(angle_gain, 2)
    return (stacked.reshape(IMG_DEV, traces, depth_len) * trace_gain[None, :, None]).astype(
        jnp.bfloat16
    )


def solution(mesh):
    placed = (
        P(("shot", "grp"), None, None),
        P(),
        P(("shot", "grp"), None),
        P(("shot", "grp"), None),
        P(("shot", "grp")),
    )
    return jax.shard_map(
        local, mesh=mesh, in_specs=placed, out_specs=P(("shot", "grp"), None, None), check_vma=False
    )
```

profile of v0, /device:TPU:9, one launch (start us, length us, event | category | flops | bytes accessed | tf_op | source)
XLA Modules:
  0.0 332.2 jit_solution(8535463626805451327)
XLA Ops:
  6.5 0.0 copy-start
  6.5 0.9 convert_reduce_fusion
  7.5 0.7 fusion.8
  8.1 0.7 convert_element_type.49
  8.8 0.9 scatter_custom_fusion
  9.7 0.7 all_to_all.16
  10.4 5.7 %all-to-all-start = ((bf16[8,1,13]{2,1,0:T(2,128)(2,1)}), bf16[8,1,13]{2,1,0:T(2,128)(2,1)S(1)}, u32[]{:S(2)}, u32[]{:S(2)}) async-start(bf16[8,1,13]{2,1,0:T(2,128)(2,1)} %all_to_all.16), calls=%async_computation | async-start | bytes 8192 | tf_op jit(solution)/shard_map/all_to_all | solution.py:69
  16.1 0.8 convert_element_type.53
  16.9 0.1 copy.10
  17.0 0.1 reshape.73
  17.1 0.8 scatter_custom_fusion.2
  18.0 0.6 reshape.48
  18.6 1.5 all-to-all-done
  20.1 4.6 %all-to-all-start.2 = ((bf16[8,13,128]{2,1,0:T(8,128)(2,1)}), bf16[8,13,128]{2,1,0:T(8,128)(2,1)S(1)}, u32[]{:S(2)}, u32[]{:S(2)}) async-start(bf16[8,13,128]{2,1,0:T(8,128)(2,1)} %reshape.48), calls=%async_computation.2 | async-start | bytes 65536 | tf_op jit(solution)/shard_map/all_to_all | solution.py:62
  24.7 3.6 %broadcast_in_dim.7 = bf16[104,2,32,512]{3,2,1,0:T(8,128)(2,1)} broadcast(bf16[]{:T(256)} %constant.2.clone.1), dimensions={} | broadcast | bytes 6815746 | tf_op jit(solution)/shard_map/broadcast_in_dim | solution.py:45
  28.3 17.6 %scatter_fusion = bf16[104,2,32,512]{3,2,1,0:T(8,128)(2,1)} fusion(bf16[104,2,32,512]{3,2,1,0:T(8,128)(2,1)} %broadcast_in_dim.7, s32[96]{0:T(128)S(1)} %fusion.8, bf16[96,2,32,512]{3,2,1,0:T(8,128)(2,1)} %bitcast.26), kind=kCustom, calls=%fused_computation.1 | custom fusion | bytes 18874752 | tf_op jit(solution)/shard_map/scatter | solution.py:47
  46.0 0.0 all-to-all-done.2
  46.0 5.4 %all-to-all-start.1 = ((bf16[8,13,2,32,512]{4,3,2,1,0:T(8,128)(2,1)}), bf16[8,13,2,32,512]{4,3,2,1,0:T(8,128)(2,1)}, u32[]{:S(2)}, u32[]{:S(2)}) async-start(bf16[8,13,2,32,512]{4,3,2,1,0:T(8,128)(2,1)} %bitcast.25), calls=%async_computation.1 | async-start | bytes 13631488 | tf_op jit(solution)/shard_map/all_to_all | solution.py:55
  51.4 0.0 all-reduce.4.cloned.1.call-start
  51.4 0.1 reshape.51
  51.5 0.1 reshape.52
  51.6 147.5 %all-to-all-done.1 = bf16[8,13,2,32,512]{4,3,2,1,0:T(8,128)(2,1)} async-done(((bf16[8,13,2,32,512]{4,3,2,1,0:T(8,128)(2,1)}), bf16[8,13,2,32,512]{4,3,2,1,0:T(8,128)(2,1)}, u32[]{:S(2)}, u32[]{:S(2)}) %all-to-all-start.1) | async-done | bytes 6815776 | tf_op jit(solution)/shard_map/all_to_all | solution.py:55
  199.0 0.0 copy-done
  199.0 10.3 %multiply_reduce_fusion = (f32[64]{0:T(128)S(1)}, bf16[208,64,512]{2,1,0:T(8,128)(2,1)}) fusion(f32[208,64]{1,0:T(8,128)S(1)} %reshape.52, bf16[208,32,512]{2,1,0:T(8,128)(2,1)} %bitcast.5, bf16[64,32]{0,1:T(8,128)(2,1)S(1)} %copy-done), kind=kOutput, calls=%fused_computation.3 | convolution fusion | flops 470286272 | bytes 20504832 | tf_op jit(solution)/shard_map/ah,phz->paz/dot_general | solution.py:10
  209.4 17.5 %reshape.49 = bf16[104,65536]{1,0:T(8,128)(2,1)} reshape(bf16[208,64,512]{2,1,0:T(8,128)(2,1)} %get-tuple-element.8) | data formatting | bytes 27262976 | tf_op jit(solution)/shard_map/reshape | solution.py:74
  226.8 0.0 copy-start.1
  226.8 8.3 %fusion.6 = f32[16,65536]{1,0:T(8,128)} fusion(bf16[104,65536]{1,0:T(8,128)(2,1)} %reshape.49, f32[104]{0:T(128)S(1)} %reshape.51), kind=kOutput, calls=%fused_computation.15 | convolution fusion | flops 218105472 | bytes 17826208 | tf_op jit(solution)/shard_map/dot_general | solution.py:82
  235.2 0.0 all-reduce.4.cloned.1.call-update
  235.2 0.0 copy-done.1
  235.2 0.6 dynamic-slice
  236.5 42.2 %all-reduce.1 = (f32[64]{0:T(128)S(1)}, f32[64]{0:T(128)S(1)}) all-reduce(f32[64]{0:T(128)S(1)} %get-tuple-element.7, f32[64]{0:T(128)S(1)} %reduce_sum.32), channel_id=1, replica_groups=mesh['shot'=8,'grp'=4] {'shot','grp'}, use_global_device_ids=true, to_apply=%region_6.0 | all-reduce | flops 128 | bytes 1024 | tf_op jit(solution)/shard_map/psum | solution.py:20
  278.7 0.1 mul.42
  278.8 43.6 %all-reduce.4.cloned.1.call-done = f32[16,65536]{1,0:T(8,128)} async-done(((f32[16,65536]{1,0:T(8,128)}), f32[16,65536]{1,0:T(8,128)}) %all-reduce.4.cloned.1.call-update) | async-done | bytes 4194320
  322.5 1.8 constant_dynamic-slice_fusion
  324.3 1.1 fusion.1
  (5 shorter events, 0.1 us)
Async XLA Ops:
  6.5 192.5 %copy-start = (bf16[64,32]{0,1:T(8,128)(2,1)S(1)}, bf16[64,32]{0,1:T(8,128)(2,1)}, u32[]{:S(2)}) copy-start(bf16[64,32]{0,1:T(8,128)(2,1)} %param.6) | copy-start | bytes 12292
  10.4 9.7 %all-to-all-start = ((bf16[8,1,13]{2,1,0:T(2,128)(2,1)}), bf16[8,1,13]{2,1,0:T(2,128)(2,1)S(1)}, u32[]{:S(2)}, u32[]{:S(2)}) async-start(bf16[8,1,13]{2,1,0:T(2,128)(2,1)} %all_to_all.16), calls=%async_computation | async-start | bytes 8192 | tf_op jit(solution)/shard_map/all_to_all | solution.py:69
  20.1 25.9 %all-to-all-start.2 = ((bf16[8,13,128]{2,1,0:T(8,128)(2,1)}), bf16[8,13,128]{2,1,0:T(8,128)(2,1)S(1)}, u32[]{:S(2)}, u32[]{:S(2)}) async-start(bf16[8,13,128]{2,1,0:T(8,128)(2,1)} %reshape.48), calls=%async_computation.2 | async-start | bytes 65536 | tf_op jit(solution)/shard_map/all_to_all | solution.py:62
  46.0 153.1 %all-to-all-start.1 = ((bf16[8,13,2,32,512]{4,3,2,1,0:T(8,128)(2,1)}), bf16[8,13,2,32,512]{4,3,2,1,0:T(8,128)(2,1)}, u32[]{:S(2)}, u32[]{:S(2)}) async-start(bf16[8,13,2,32,512]{4,3,2,1,0:T(8,128)(2,1)} %bitcast.25), calls=%async_computation.1 | async-start | bytes 13631488 | tf_op jit(solution)/shard_map/all_to_all | solution.py:55
  51.4 271.1 %all-reduce.4.cloned.1.call-start = ((), (), s32[]{:S(2)}) async-start(), calls=%async_computation.3 | async-start | bytes 8388608
  226.8 8.4 %copy-start.1 = (u32[32]{0:T(128)S(1)}, u32[32]{0:T(128)}, u32[]{:S(2)}) copy-start(u32[32]{0:T(128)} %constant.20) | copy-start | bytes 388
Sparse Core Ops, SparseCore 0:
  235.3 87.1 all-reduce.3
where the time goes:
time: 335 us; the launch traced here: 332 us
  waiting for transfers between devices  193 us (58%)
  local copies, waits for them, and re-layouts  44.6 us (13%)
  blocking collectives  42.2 us (13%)
  matrix products  18.7 us (6%)
  starting transfers between devices  15.8 us (5%)
  between operations  14.1 us (4%)
  other arithmetic  4.28 us (1%)
    all_to_all x1, waiting for transfers between devices, local(): lax.all_to_all(raw_sent.reshape((peer_count, capacity, 2) + inner), 'shot...  147 us
    unnamed x2, waiting for transfers between devices  43.7 us
    psum x1, blocking collectives, global_gain(): totals = lax.psum((square_sum, live_count), ('shot', 'grp'))  42.2 us
    scatter x1, local copies, waits for them, and re-layouts, local(): raw_sent = jnp.zeros((slot_count, 2) + inner, jnp.bfloat16).at[targets].s...  17.6 us
    reshape x1, local copies, waits for them, and re-layouts, local(): received = angles.reshape(slot_count, traces * depth_len)  17.5 us
    dot_general x1, matrix products, slant_stack(): jnp.einsum('ah,phz->paz', weights, gathers, preferred_element_type=jnp.fl...  10.3 us
    dot_general x1, matrix products, local(): jnp.dot(holder, received, preferred_element_type=jnp.float32)  8.33 us
  transfers between devices with their start and end apart: 4, of which 3 were waited for; matrix products, arithmetic and copies ran while one was open for 7% of the time, Pallas kernels for 0%

commit v1 on v0

v1 whole, which is shorter than its diff:
```python
import functools

import jax
import jax.numpy as jnp
from jax import lax
from jax.experimental import pallas as pl
from jax.experimental.pallas import tpu as pltpu
from jax.sharding import PartitionSpec as P

IMG_DEV = 4
PAIR = 2
LANES = 128
UNROLL = 8
MESH = pl.DeviceIdType.MESH


def place(grp):
    shot, g = lax.axis_index("shot"), lax.axis_index("grp")
    return lax.div(shot, PAIR), lax.rem(shot, PAIR) * grp + g


def at(plane, spot, grp):
    return (plane * PAIR + lax.div(spot, grp), lax.rem(spot, grp))


def share(spot, width, depth):
    start = spot * width
    return lax.div(start, depth), pl.multiple_of(lax.rem(start, depth), LANES)


def exchange_kernel(grp, off, aux, raw_in, aux_in, stage, send, recv, asend, arecv, lsem):
    size = PAIR * grp
    plane, spot = place(grp)
    depth, width = off.shape[3], raw_in.shape[3]
    barrier = pltpu.get_barrier_semaphore()
    for r in range(1, size):
        pl.semaphore_signal(
            barrier, inc=1, device_id=at(plane, lax.rem(spot + r, size), grp), device_id_type=MESH
        )
    pl.semaphore_wait(barrier, size - 1)
    copies = []
    for r in range(1, size):
        peer = lax.rem(spot + r, size)
        j, first = share(peer, width, depth)
        dev = at(plane, peer, grp)
        copies.append(
            pltpu.make_async_remote_copy(
                src_ref=aux,
                dst_ref=aux_in.at[spot],
                send_sem=asend.at[r - 1],
                recv_sem=arecv.at[r - 1],
                device_id=dev,
                device_id_type=MESH,
            )
        )
        copies.append(
            pltpu.make_async_remote_copy(
                src_ref=off.at[:, j, :, pl.ds(first, width)],
                dst_ref=raw_in.at[spot],
                send_sem=send.at[r - 1],
                recv_sem=recv.at[r - 1],
                device_id=dev,
                device_id_type=MESH,
            )
        )
    for copy in copies:
        copy.start()
    j, first = share(spot, width, depth)
    a = pltpu.make_async_copy(off.at[:, j, :, pl.ds(first, width)], stage, lsem.at[0])
    c = pltpu.make_async_copy(aux, aux_in.at[spot], lsem.at[1])
    a.start()
    c.start()
    a.wait()
    b = pltpu.make_async_copy(stage, raw_in.at[spot], lsem.at[2])
    b.start()
    b.wait()
    c.wait()
    for copy in copies:
        copy.wait()


def stack_kernel(steps, half, aux, w, raw, part, mom, acc, sums):
    c, s = pl.program_id(0), pl.program_id(1)
    angles = w.shape[0]

    @pl.when(s == 0)
    def _():
        acc[...] = jnp.zeros_like(acc)

    @pl.when((s == 0) & (c == 0))
    def _():
        sums[...] = jnp.zeros_like(sums)

    @pl.when(s < steps)
    def _():
        row = lax.broadcasted_iota(jnp.int32, (angles, LANES), 0)
        weights = w[...]
        mine = 1 + half[0]

        def body(i, carry):
            square, count = carry
            first = i * UNROLL
            x = jnp.concatenate([raw[0, first + t] for t in range(UNROLL)], axis=1)
            y = jnp.dot(weights, x, preferred_element_type=jnp.float32)
            for t in range(UNROLL):
                alive = row < aux[s, mine, first + t]
                slanted = jnp.where(alive, y[:, t * LANES : (t + 1) * LANES], 0.0)
                slanted = slanted.astype(jnp.bfloat16).astype(jnp.float32)
                square += slanted * slanted
                count += jnp.where(alive, 1.0, 0.0)
                k = aux[s, 0, first + t]
                acc[k] += slanted
            return square, count

        square, count = lax.fori_loop(0, raw.shape[1] // UNROLL, body, (sums[0], sums[1]))
        sums[0] = square
        sums[1] = count

    @pl.when(s >= steps)
    def _():
        rows = part.shape[0]
        part[...] = acc[pl.ds((s - steps) * rows, rows)].astype(jnp.bfloat16)
        lane = lax.broadcasted_iota(jnp.int32, (angles, LANES), 1)
        square = jnp.sum(sums[0], axis=1, keepdims=True)
        count = jnp.sum(sums[1], axis=1, keepdims=True)
        mom[...] = jnp.where(lane == 0, square, jnp.where(lane == 1, count, 0.0))


def gather_kernel(
    grp, part, mom, out, zin, own, fin, pin, qin, half_sum, zs, zr, ps, pr, qs, qr, fs, fr, lsem
):
    size = PAIR * grp
    planes = zin.shape[0] + 1
    plane, spot = place(grp)
    rows, width, depth = own.shape[0], own.shape[2], out.shape[2]
    angles = own.shape[1]
    barrier = pltpu.get_barrier_semaphore()
    for r in range(1, size):
        pl.semaphore_signal(
            barrier, inc=1, device_id=at(plane, lax.rem(spot + r, size), grp), device_id_type=MESH
        )
    for r in range(1, planes):
        pl.semaphore_signal(
            barrier, inc=1, device_id=at(lax.rem(plane + r, planes), spot, grp), device_id_type=MESH
        )
    pl.semaphore_wait(barrier, size + planes - 2)

    near = [
        pltpu.make_async_remote_copy(
            src_ref=mom,
            dst_ref=pin.at[r - 1],
            send_sem=ps.at[r - 1],
            recv_sem=pr.at[r - 1],
            device_id=at(plane, lax.rem(spot + r, size), grp),
            device_id_type=MESH,
        )
        for r in range(1, size)
    ]
    for copy in near:
        copy.start()
    mine = pltpu.make_async_copy(part.at[pl.ds(plane * rows, rows)], own, lsem.at[0])
    mine.start()
    far = []
    for r in range(1, planes):
        target = lax.rem(plane + r, planes)
        far.append(
            pltpu.make_async_remote_copy(
                src_ref=part.at[pl.ds(target * rows, rows)],
                dst_ref=zin.at[r - 1],
                send_sem=zs.at[r - 1],
                recv_sem=zr.at[r - 1],
                device_id=at(target, spot, grp),
                device_id_type=MESH,
            )
        )
    total = mom[...]
    for copy in near:
        copy.wait()
    for r in range(1, size):
        total += pin[r - 1]
    half_sum[...] = total
    wide = [
        pltpu.make_async_remote_copy(
            src_ref=half_sum,
            dst_ref=qin.at[r - 1],
            send_sem=qs.at[r - 1],
            recv_sem=qr.at[r - 1],
            device_id=at(lax.rem(plane + r, planes), spot, grp),
            device_id_type=MESH,
        )
        for r in range(1, planes)
    ]
    for copy in wide:
        copy.start()
    for copy in far:
        copy.start()
    for copy in wide:
        copy.wait()
    total = half_sum[...]
    for r in range(1, planes):
        total += qin[r - 1]
    gain = lax.rsqrt(total[:, 0:1] / total[:, 1:2] + 1e-06)
    gain = jnp.broadcast_to(gain, (angles, width))
    mine.wait()
    for copy in far:
        copy.wait()

    def body(i, _):
        value = own[i].astype(jnp.float32)
        for r in range(1, planes):
            value += zin[r - 1, i].astype(jnp.float32)
        fin[i] = (value * gain).astype(jnp.bfloat16)
        return 0

    lax.fori_loop(0, rows, body, 0)

    each = rows // size
    j, first = share(spot, width, depth)
    view = out.at[:, pl.ds(pl.multiple_of(j * angles, angles), angles), pl.ds(first, width)]
    last = pltpu.make_async_copy(fin.at[pl.ds(spot * each, each)], view, lsem.at[1])
    final = []
    for r in range(1, size):
        peer = lax.rem(spot + r, size)
        final.append(
            pltpu.make_async_remote_copy(
                src_ref=fin.at[pl.ds(peer * each, each)],
                dst_ref=view,
                send_sem=fs.at[r - 1],
                recv_sem=fr.at[r - 1],
                device_id=at(plane, peer, grp),
                device_id_type=MESH,
            )
        )
    for copy in final:
        copy.start()
    last.start()
    last.wait()
    for copy in final:
        copy.wait()


def local(offsets, slant_weights, live, block_tile, image_slot):
    shots, grp = lax.axis_size("shot"), lax.axis_size("grp")
    planes, size = shots // PAIR, PAIR * grp
    blocks = block_tile.shape[0]
    hs, depth = offsets.shape[1:]
    angles = slant_weights.shape[0]
    width = 2 * depth // size
    tile_rows = IMG_DEV * grp
    images = shots * tile_rows
    per_plane = images // planes
    any_space = pl.BlockSpec(memory_space=pl.ANY)
    vmem = pl.BlockSpec(memory_space=pltpu.VMEM)
    smem = pl.BlockSpec(memory_space=pltpu.SMEM)
    dma = pltpu.SemaphoreType.DMA

    cutoff = jnp.sum(live.reshape(blocks, 2, angles), axis=2)
    image = block_tile[:, 0] * tile_rows + image_slot
    aux = jnp.concatenate([image[None], cutoff.T], axis=0)
    aux = jnp.pad(aux, ((0, 5), (0, -blocks % LANES)))

    raw_in, aux_in = pl.pallas_call(
        functools.partial(exchange_kernel, grp),
        out_shape=(
            jax.ShapeDtypeStruct((size, blocks, hs, width), jnp.bfloat16),
            jax.ShapeDtypeStruct((size,) + aux.shape, jnp.int32),
        ),
        in_specs=[any_space, vmem],
        out_specs=(any_space, vmem),
        scratch_shapes=[
            pltpu.VMEM((blocks, hs, width), jnp.bfloat16),
            dma((size - 1,)),
            dma((size - 1,)),
            dma((size - 1,)),
            dma((size - 1,)),
            dma((3,)),
        ],
        compiler_params=pltpu.CompilerParams(collective_id=0, has_side_effects=True),
        name="exchange",
    )(offsets.reshape(blocks, 2, hs, depth), aux)

    spot = lax.rem(lax.axis_index("shot"), PAIR) * grp + lax.axis_index("grp")
    half = (spot * width // depth).astype(jnp.int32).reshape(1)
    part, mom = pl.pallas_call(
        functools.partial(stack_kernel, size),
        grid=(width // LANES, size + planes),
        out_shape=(
            jax.ShapeDtypeStruct((images, angles, width), jnp.bfloat16),
            jax.ShapeDtypeStruct((angles, LANES), jnp.float32),
        ),
        in_specs=[
            smem,
            smem,
            pl.BlockSpec((angles, hs), lambda c, s: (0, 0)),
            pl.BlockSpec(
                (1, blocks, hs, LANES), lambda c, s: (jnp.minimum(s, size - 1), 0, 0, c)
            ),
        ],
        out_specs=(
            pl.BlockSpec(
                (per_plane, angles, LANES), lambda c, s: (jnp.maximum(s - size, 0), 0, c)
            ),
            pl.BlockSpec((angles, LANES), lambda c, s: (0, 0)),
        ),
        scratch_shapes=[
            pltpu.VMEM((images, angles, LANES), jnp.float32),
            pltpu.VMEM((2, angles, LANES), jnp.float32),
        ],
        compiler_params=pltpu.CompilerParams(vmem_limit_bytes=60 * 1024 * 1024),
        name="stack",
    )(half, aux_in, slant_weights, raw_in)

    moments = (angles, LANES)
    return pl.pallas_call(
        functools.partial(gather_kernel, grp),
        out_shape=jax.ShapeDtypeStruct((IMG_DEV, 2 * angles, depth), jnp.bfloat16),
        in_specs=[any_space, vmem],
        out_specs=any_space,
        scratch_shapes=[
            pltpu.VMEM((planes - 1, per_plane, angles, width), jnp.bfloat16),
            pltpu.VMEM((per_plane, angles, width), jnp.bfloat16),
            pltpu.VMEM((per_plane, angles, width), jnp.bfloat16),
            pltpu.VMEM((size - 1,) + moments, jnp.float32),
            pltpu.VMEM((planes - 1,) + moments, jnp.float32),
            pltpu.VMEM(moments, jnp.float32),
            dma((planes - 1,)),
            dma((planes - 1,)),
            dma((size - 1,)),
            dma((size - 1,)),
            dma((planes - 1,)),
            dma((planes - 1,)),
            dma((size - 1,)),
            dma((size - 1,)),
            dma((2,)),
        ],
        compiler_params=pltpu.CompilerParams(
            collective_id=1, has_side_effects=True, vmem_limit_bytes=60 * 1024 * 1024
        ),
        name="gather",
    )(part, mom)


def solution(mesh):
    placed = (
        P(("shot", "grp"), None, None),
        P(),
        P(("shot", "grp"), None),
        P(("shot", "grp"), None),
        P(("shot", "grp")),
    )
    return jax.shard_map(
        local, mesh=mesh, in_specs=placed, out_specs=P(("shot", "grp"), None, None), check_vma=False
    )
```

time: 335 us -> 168 us (0.50)
  waiting for transfers between devices: 193 us -> 0 us
  Pallas kernels: 0 us -> 162 us
  blocking collectives: 42.2 us -> 0 us
  local copies, waits for them, and re-layouts: 44.6 us -> 4.05 us
  matrix products: 18.7 us -> 0 us
  starting transfers between devices: 15.8 us -> 0 us
  between operations: 14.1 us -> 0.03 us
    pallas_call x0 -> x3, Pallas kernels: none -> 162 us  [the longest x1 73.6 us: local(): pl.pallas_call(functools.partial(exchange_kernel, grp), out_shape=(jax.Sh...]
    all_to_all x3 -> x0, waiting for transfers between devices: 149 us -> none  [the longest x1 147 us: local(): lax.all_to_all(raw_sent.reshape((peer_count, capacity, 2) + inner), 'shot...]
    unnamed x2 -> x0, waiting for transfers between devices: 43.7 us -> none
    psum x1 -> x0, blocking collectives: 42.2 us -> none  [global_gain(): totals = lax.psum((square_sum, live_count), ('shot', 'grp'))]
    scatter x3 -> x0, local copies, waits for them, and re-layouts: 19.3 us -> none  [the longest x1 17.6 us: local(): raw_sent = jnp.zeros((slot_count, 2) + inner, jnp.bfloat16).at[targets].s...]
    dot_general x2 -> x0, matrix products: 18.7 us -> none  [the longest x1 10.3 us: slant_stack(): jnp.einsum('ah,phz->paz', weights, gathers, preferred_element_type=jnp.fl...]
    reshape x2 -> x0, local copies, waits for them, and re-layouts: 18.1 us -> none  [the longest x1 17.5 us: local(): received = angles.reshape(slot_count, traces * depth_len)]
    all_to_all x3 -> x0, starting transfers between devices: 15.8 us -> none  [the longest x1 5.72 us: local(): lax.all_to_all(labels, 'shot', split_axis=0, concat_axis=0, tiled=True)]
  transfers between devices with their start and end apart: 4 -> 0, of which waited for: 3 -> 0; matrix products, arithmetic and copies ran while one was open for 7% -> 0% of each run, Pallas kernels for 0% -> 0%
where the time goes in v1:
time: 168 us
  Pallas kernels  162 us (96%)
  local copies, waits for them, and re-layouts  4.05 us (2%)
    pallas_call x1, Pallas kernels, local(): pl.pallas_call(functools.partial(exchange_kernel, grp), out_shape=(jax.Sh...  73.6 us
    pallas_call x1, Pallas kernels, local(): pl.pallas_call(functools.partial(gather_kernel, grp), out_shape=jax.Shape...  65.5 us
    pallas_call x1, Pallas kernels, local(): pl.pallas_call(functools.partial(stack_kernel, size), grid=(width // LANE...  23.2 us

profile of v1, /device:TPU:9, one launch (start us, length us, event | category | flops | bytes accessed | tf_op | source)
XLA Modules:
  0.0 168.0 jit_solution(10331500527268583496)
XLA Ops:
  0.0 0.7 fusion
  0.7 0.9 reduce_sum.11
  1.5 1.4 copy.8.w
  2.9 0.1 reduce_sum.12
  3.1 0.1 copy.7
  3.1 0.6 pad.4.aux
  3.8 73.6 %exchange.1 = (bf16[8,96,32,128]{3,2,1,0:T(8,128)(2,1)}, s32[8,8,128]{2,1,0:T(8,128)}) custom-call(bf16[96,2,32,512]{3,2,1,0:T(8,128)(2,1)} %bitcast.9, s32[8,128]{1,0:T(8,128)} %pad.4.aux), custom_call_target="tpu_custom_call" | custom-call | tf_op jit(solution)/shard_map/exchange/pallas_call | solution.py:262
  77.3 23.2 %stack.1 = (bf16[128,64,128]{2,1,0:T(8,128)(2,1)}, f32[64,128]{1,0:T(8,128)}) custom-call(s32[1]{0:T(128)} %bitcast.half, s32[8,8,128]{2,1,0:T(8,128)} %get-tuple-element.9.aux, bf16[64,32]{1,0:T(8,128)(2,1)} %copy.8.w, bf16[8,96,32,128]{3,2,1,0:T(8,128)(2,1)} %get-tuple-element.10.raw), custom_call_target="tpu_custom_call" | custom-call | tf_op jit(solution)/shard_map/stack/pallas_call | solution.py:284
  100.6 65.5 %gather.1 = bf16[4,128,512]{2,1,0:T(8,128)(2,1)} custom-call(bf16[128,64,128]{2,1,0:T(8,128)(2,1)} %get-tuple-element.11.part, f32[64,128]{1,0:T(8,128)} %get-tuple-element.12.mom), custom_call_target="tpu_custom_call" | custom-call | tf_op jit(solution)/shard_map/gather/pallas_call | solution.py:314
  166.1 1.9 %copy.10 = bf16[4,128,512]{2,1,0:T(8,128)(2,1)} copy(bf16[4,128,512]{2,1,0:T(8,128)(2,1)} %gather.1) | data formatting | bytes 1048576
  (1 shorter events, 0.0 us)

commit v2 on v1

--- a/solution.py
+++ b/solution.py
@@ -28,102 +28,123 @@
     return lax.div(start, depth), pl.multiple_of(lax.rem(start, depth), LANES)
 
 
-def exchange_kernel(grp, off, aux, raw_in, aux_in, stage, send, recv, asend, arecv, lsem):
+def relative(spot, grp, r):
+    mid = grp // 2
+    pair, rest = lax.div(spot, grp), lax.rem(spot, grp)
+    m, c = lax.div(rest, 2), lax.rem(rest, 2)
+    rp, rm, rc = r // grp, (r % grp) // 2, r % 2
+    pair, m, c = lax.rem(pair + rp, PAIR), lax.rem(m + rm, mid), lax.rem(c + rc, 2)
+    return (pair * mid + m) * 2 + c
+
+
+def orders(grp):
+    size = PAIR * grp
+    far = list(range(grp + 2, size))
+    side = list(range(grp, grp + 2))
+    ahead = list(range(2, grp))
+    turn = []
+    for i in range(max(len(far), len(ahead))):
+        for group in (far, side, ahead):
+            turn += group[i : i + 1]
+    return [1] + turn
+
+
+def exchange_kernel(
+    grp, off, aux, w, part, mom, raw, aux_in, codes, acc, seg, send, recv, asend, arecv, lsem
+):
     size = PAIR * grp
     plane, spot = place(grp)
-    depth, width = off.shape[3], raw_in.shape[3]
+    blocks, depth, width = off.shape[0], off.shape[3], raw.shape[3]
+    angles, images = w.shape[0], acc.shape[0]
+    j, first = share(spot, width, depth)
+    mine = pltpu.make_async_copy(off.at[:, j, :, pl.ds(first, width)], raw.at[0], lsem.at[0])
+    mine.start()
+    own_codes = pltpu.make_async_copy(aux, codes.at[0], lsem.at[1])
+    own_codes.start()
     barrier = pltpu.get_barrier_semaphore()
     for r in range(1, size):
         pl.semaphore_signal(
-            barrier, inc=1, device_id=at(plane, lax.rem(spot + r, size), grp), device_id_type=MESH
+            barrier, inc=1, device_id=at(plane, relative(spot, grp, r), grp), device_id_type=MESH
         )
     pl.semaphore_wait(barrier, size - 1)
-    copies = []
-    for r in range(1, size):
-        peer = lax.rem(spot + r, size)
-        j, first = share(peer, width, depth)
+    data, notes = {}, {}
+    for r in orders(grp):
+        peer = relative(spot, grp, r)
+        pj, pfirst = share(peer, width, depth)
         dev = at(plane, peer, grp)
-        copies.append(
-            pltpu.make_async_remote_copy(
-                src_ref=aux,
-                dst_ref=aux_in.at[spot],
-                send_sem=asend.at[r - 1],
-                recv_sem=arecv.at[r - 1],
-                device_id=dev,
-                device_id_type=MESH,
-            )
-        )
-        copies.append(
-            pltpu.make_async_remote_copy(
-                src_ref=off.at[:, j, :, pl.ds(first, width)],
-                dst_ref=raw_in.at[spot],
-                send_sem=send.at[r - 1],
-                recv_sem=recv.at[r - 1],
-                device_id=dev,
-                device_id_type=MESH,
-            )
-        )
-    for copy in copies:
-        copy.start()
-    j, first = share(spot, width, depth)
-    a = pltpu.make_async_copy(off.at[:, j, :, pl.ds(first, width)], stage, lsem.at[0])
-    c = pltpu.make_async_copy(aux, aux_in.at[spot], lsem.at[1])
-    a.start()
-    c.start()
-    a.wait()
-    b = pltpu.make_async_copy(stage, raw_in.at[spot], lsem.at[2])
-    b.start()
-    b.wait()
-    c.wait()
-    for copy in copies:
-        copy.wait()
-
-
-def stack_kernel(steps, half, aux, w, raw, part, mom, acc, sums):
-    c, s = pl.program_id(0), pl.program_id(1)
-    angles = w.shape[0]
-
-    @pl.when(s == 0)
-    def _():
-        acc[...] = jnp.zeros_like(acc)
-
-    @pl.when((s == 0) & (c == 0))
-    def _():
-        sums[...] = jnp.zeros_like(sums)
-
-    @pl.when(s < steps)
-    def _():
-        row = lax.broadcasted_iota(jnp.int32, (angles, LANES), 0)
-        weights = w[...]
-        mine = 1 + half[0]
-
-        def body(i, carry):
+        notes[r] = pltpu.make_async_remote_copy(
+            src_ref=aux,
+            dst_ref=aux_in.at[r],
+            send_sem=asend.at[r - 1],
+            recv_sem=arecv.at[r - 1],
+            device_id=dev,
+            device_id_type=MESH,
+        )
+        data[r] = pltpu.make_async_remote_copy(
+            src_ref=off.at[:, pj, :, pl.ds(pfirst, width)],
+            dst_ref=raw.at[r],
+            send_sem=send.at[r - 1],
+            recv_sem=recv.at[r - 1],
+            device_id=dev,
+            device_id_type=MESH,
+        )
+    for r in orders(grp):
+        notes[r].start()
+    for r in orders(grp):
+        data[r].start()
+
+    acc[...] = jnp.zeros_like(acc)
+    seg[blocks] = jnp.zeros((angles, width), jnp.float32)
+    row = lax.broadcasted_iota(jnp.int32, (angles, width), 0)
+    weights = w[...]
+    square = jnp.zeros((angles, width), jnp.float32)
+    count = jnp.zeros((angles, width), jnp.float32)
+    for r in [0] + orders(grp):
+        if r:
+            notes[r].wait()
+            code = pltpu.make_async_copy(aux_in.at[r], codes.at[r], lsem.at[r + 1])
+            code.start()
+            code.wait()
+            data[r].wait()
+        else:
+            own_codes.wait()
+            mine.wait()
+
+        def slant(i, carry, r=r):
             square, count = carry
-            first = i * UNROLL
-            x = jnp.concatenate([raw[0, first + t] for t in range(UNROLL)], axis=1)
+            start = i * UNROLL
+            x = jnp.concatenate([raw[r, start + t] for t in range(UNROLL)], axis=1)
             y = jnp.dot(weights, x, preferred_element_type=jnp.float32)
             for t in range(UNROLL):
-                alive = row < aux[s, mine, first + t]
-                slanted = jnp.where(alive, y[:, t * LANES : (t + 1) * LANES], 0.0)
+                alive = row < codes[r, 1 + j, start + t]
+                slanted = jnp.where(alive, y[:, t * width : (t + 1) * width], 0.0)
                 slanted = slanted.astype(jnp.bfloat16).astype(jnp.float32)
                 square += slanted * slanted
                 count += jnp.where(alive, 1.0, 0.0)
-                k = aux[s, 0, first + t]
-                acc[k] += slanted
+                seg[start + t] = slanted + seg[codes[r, 0, start + t]]
             return square, count
 
-        square, count = lax.fori_loop(0, raw.shape[1] // UNROLL, body, (sums[0], sums[1]))
-        sums[0] = square
-        sums[1] = count
-
-    @pl.when(s >= steps)
-    def _():
-        rows = part.shape[0]
-        part[...] = acc[pl.ds((s - steps) * rows, rows)].astype(jnp.bfloat16)
-        lane = lax.broadcasted_iota(jnp.int32, (angles, LANES), 1)
-        square = jnp.sum(sums[0], axis=1, keepdims=True)
-        count = jnp.sum(sums[1], axis=1, keepdims=True)
-        mom[...] = jnp.where(lane == 0, square, jnp.where(lane == 1, count, 0.0))
+        square, count = lax.fori_loop(0, blocks // UNROLL, slant, (square, count))
+
+        def stack(i, _, r=r):
+            start = i * UNROLL
+            line, column = lax.div(start, LANES), lax.rem(start, LANES)
+            for t in range(UNROLL):
+                acc[start + t] += seg[codes[r, 3 + line, column + t]]
+            return 0
+
+        lax.fori_loop(0, images // UNROLL, stack, 0)
+
+    def narrow(i, _):
+        start = pl.multiple_of(i * UNROLL, UNROLL)
+        part[pl.ds(start, UNROLL)] = acc[pl.ds(start, UNROLL)].astype(jnp.bfloat16)
+        return 0
+
+    lax.fori_loop(0, images // UNROLL, narrow, 0)
+    lane = lax.broadcasted_iota(jnp.int32, (angles, LANES), 1)
+    square = jnp.sum(square, axis=1, keepdims=True)
+    count = jnp.sum(count, axis=1, keepdims=True)
+    mom[...] = jnp.where(lane == 0, square, jnp.where(lane == 1, count, 0.0))
 
 
 def gather_kernel(
@@ -173,6 +194,8 @@
                 device_id_type=MESH,
             )
         )
+    for copy in far:
+        copy.start()
     total = mom[...]
     for copy in near:
         copy.wait()
@@ -191,8 +214,6 @@
         for r in range(1, planes)
     ]
     for copy in wide:
-        copy.start()
-    for copy in far:
         copy.start()
     for copy in wide:
         copy.wait()
@@ -251,64 +272,46 @@
     per_plane = images // planes
     any_space = pl.BlockSpec(memory_space=pl.ANY)
     vmem = pl.BlockSpec(memory_space=pltpu.VMEM)
-    smem = pl.BlockSpec(memory_space=pltpu.SMEM)
     dma = pltpu.SemaphoreType.DMA
 
     cutoff = jnp.sum(live.reshape(blocks, 2, angles), axis=2)
     image = block_tile[:, 0] * tile_rows + image_slot
-    aux = jnp.concatenate([image[None], cutoff.T], axis=0)
-    aux = jnp.pad(aux, ((0, 5), (0, -blocks % LANES)))
-
-    raw_in, aux_in = pl.pallas_call(
+    index = jnp.arange(blocks, dtype=jnp.int32)
+    same = (image[:, None] == image[None, :]) & (index[None, :] < index[:, None])
+    before = jnp.max(jnp.where(same, index[None, :], -1), axis=1)
+    found = image[None, :] == jnp.arange(images, dtype=jnp.int32)[:, None]
+    final = jnp.max(jnp.where(found, index[None, :], -1), axis=1)
+    final = jnp.where(final < 0, blocks, final).reshape(images // LANES, LANES)
+    before = jnp.where(before < 0, blocks, before)
+    aux = jnp.concatenate([before[None], cutoff.T], axis=0)
+    aux = jnp.concatenate([jnp.pad(aux, ((0, 0), (0, LANES - blocks))), final], axis=0)
+    aux = jnp.pad(aux, ((0, -aux.shape[0] % 8), (0, 0)))
+
+    part, mom = pl.pallas_call(
         functools.partial(exchange_kernel, grp),
-        out_shape=(
-            jax.ShapeDtypeStruct((size, blocks, hs, width), jnp.bfloat16),
-            jax.ShapeDtypeStruct((size,) + aux.shape, jnp.int32),
-        ),
-        in_specs=[any_space, vmem],
-        out_specs=(any_space, vmem),
-        scratch_shapes=[
-            pltpu.VMEM((blocks, hs, width), jnp.bfloat16),
-            dma((size - 1,)),
-            dma((size - 1,)),
-            dma((size - 1,)),
-            dma((size - 1,)),
-            dma((3,)),
-        ],
-        compiler_params=pltpu.CompilerParams(collective_id=0, has_side_effects=True),
-        name="exchange",
-    )(offsets.reshape(blocks, 2, hs, depth), aux)
-
-    spot = lax.rem(lax.axis_index("shot"), PAIR) * grp + lax.axis_index("grp")
-    half = (spot * width // depth).astype(jnp.int32).reshape(1)
-    part, mom = pl.pallas_call(
-        functools.partial(stack_kernel, size),
-        grid=(width // LANES, size + planes),
         out_shape=(
             jax.ShapeDtypeStruct((images, angles, width), jnp.bfloat16),
             jax.ShapeDtypeStruct((angles, LANES), jnp.float32),
         ),
-        in_specs=[
-            smem,
-            smem,
-            pl.BlockSpec((angles, hs), lambda c, s: (0, 0)),
-            pl.BlockSpec(
-                (1, blocks, hs, LANES), lambda c, s: (jnp.minimum(s, size - 1), 0, 0, c)
-            ),
+        in_specs=[any_space, vmem, vmem],
+        out_specs=(vmem, vmem),
+        scratch_shapes=[
+            pltpu.VMEM((size, blocks, hs, width), jnp.bfloat16),
+            pltpu.VMEM((size,) + aux.shape, jnp.int32),
+            pltpu.SMEM((size,) + aux.shape, jnp.int32),
+            pltpu.VMEM((images, angles, width), jnp.float32),
+            pltpu.VMEM((blocks + 1, angles, width), jnp.float32),
+            dma((size - 1,)),
+            dma((size - 1,)),
+            dma((size - 1,)),
+            dma((size - 1,)),
+            dma((size + 1,)),
         ],
-        out_specs=(
-            pl.BlockSpec(
-                (per_plane, angles, LANES), lambda c, s: (jnp.maximum(s - size, 0), 0, c)
-            ),
-            pl.BlockSpec((angles, LANES), lambda c, s: (0, 0)),
+        compiler_params=pltpu.CompilerParams(
+            collective_id=0, has_side_effects=True, vmem_limit_bytes=62 * 1024 * 1024
         ),
-        scratch_shapes=[
-            pltpu.VMEM((images, angles, LANES), jnp.float32),
-            pltpu.VMEM((2, angles, LANES), jnp.float32),
-        ],
-        compiler_params=pltpu.CompilerParams(vmem_limit_bytes=60 * 1024 * 1024),
-        name="stack",
-    )(half, aux_in, slant_weights, raw_in)
+        name="exchange",
+    )(offsets.reshape(blocks, 2, hs, depth), aux, slant_weights)
 
     moments = (angles, LANES)
     return pl.pallas_call(

time: 168 us -> 149 us (0.89)
  Pallas kernels: 162 us -> 142 us
    pallas_call x1 -> x0, Pallas kernels: 23.2 us -> none  [local(): pl.pallas_call(functools.partial(stack_kernel, size), grid=(width // LANE...]
    pallas_call x1, Pallas kernels: 73.6 us -> 81 us  [local(): pl.pallas_call(functools.partial(exchange_kernel, grp), out_shape=(jax.Sh...]
    pallas_call x1, Pallas kernels: 65.5 us -> 60.9 us  [local(): pl.pallas_call(functools.partial(gather_kernel, grp), out_shape=jax.Shape...]
where the time goes in v2:
time: 149 us; the launch traced here: 148 us
  Pallas kernels  142 us (95%)
  local copies, waits for them, and re-layouts  4.06 us (3%)
  other arithmetic  1.86 us (1%)
    pallas_call x1, Pallas kernels, local(): pl.pallas_call(functools.partial(exchange_kernel, grp), out_shape=(jax.Sh...  81 us
    pallas_call x1, Pallas kernels, local(): pl.pallas_call(functools.partial(gather_kernel, grp), out_shape=jax.Shape...  60.9 us
    unnamed x2, local copies, waits for them, and re-layouts  3.26 us

profile of v2, /device:TPU:9, one launch (start us, length us, event | category | flops | bytes accessed | tf_op | source)
XLA Modules:
  0.0 147.9 jit_solution(8021508185469140546)
XLA Ops:
  0.0 0.7 bitcast_add_fusion
  0.7 0.2 select_reduce_fusion.1
  0.9 0.1 select_reduce_fusion
  1.0 0.9 reduce_sum.11
  1.8 1.4 copy.10.w
  3.2 0.1 reduce_sum.12
  3.4 0.1 copy.9
  3.5 0.6 pad.9.aux
  4.1 81.0 %exchange.1 = (bf16[128,64,128]{2,1,0:T(8,128)(2,1)}, f32[64,128]{1,0:T(8,128)}) custom-call(bf16[96,2,32,512]{3,2,1,0:T(8,128)(2,1)} %bitcast.8, s32[8,128]{1,0:T(8,128)} %pad.9.aux, bf16[64,32]{1,0:T(8,128)(2,1)} %copy.10.w), custom_call_target="tpu_custom_call" | custom-call | tf_op jit(solution)/shard_map/exchange/pallas_call | solution.py:290
  85.1 60.9 %gather.1 = bf16[4,128,512]{2,1,0:T(8,128)(2,1)} custom-call(bf16[128,64,128]{2,1,0:T(8,128)(2,1)} %get-tuple-element.7.part, f32[64,128]{1,0:T(8,128)} %get-tuple-element.8.mom), custom_call_target="tpu_custom_call" | custom-call | tf_op jit(solution)/shard_map/gather/pallas_call | solution.py:317
  146.0 1.9 %copy.12 = bf16[4,128,512]{2,1,0:T(8,128)(2,1)} copy(bf16[4,128,512]{2,1,0:T(8,128)(2,1)} %gather.1) | data formatting | bytes 1048576
  (4 shorter events, 0.0 us)

commit v3 on v2

--- a/solution.py
+++ b/solution.py
@@ -144,17 +144,21 @@
     lane = lax.broadcasted_iota(jnp.int32, (angles, LANES), 1)
     square = jnp.sum(square, axis=1, keepdims=True)
     count = jnp.sum(count, axis=1, keepdims=True)
-    mom[...] = jnp.where(lane == 0, square, jnp.where(lane == 1, count, 0.0))
+    both = jnp.where(lane == 0, square, jnp.where(lane == 1, count, 0.0))
+    both = jnp.concatenate([both, jnp.zeros((LANES - angles, LANES), jnp.float32)], axis=0)
+    mom[...] = both.T[: mom.shape[0]]
 
 
 def gather_kernel(
-    grp, part, mom, out, zin, own, fin, pin, qin, half_sum, zs, zr, ps, pr, qs, qr, fs, fr, lsem
+    grp, part, mom, out, held, total, fin, pin, qin, half_sum, zs, zr, ps, pr, qs, qr, fs, fr, lsem
 ):
     size = PAIR * grp
-    planes = zin.shape[0] + 1
+    planes = held.shape[1] + 1
     plane, spot = place(grp)
-    rows, width, depth = own.shape[0], own.shape[2], out.shape[2]
-    angles = own.shape[1]
+    pieces, rows, angles, width = held.shape[2:]
+    depth = out.shape[2]
+    chunk = pieces * rows
+    lower = jnp.where(plane < planes // 2, 1, 0)
     barrier = pltpu.get_barrier_semaphore()
     for r in range(1, size):
         pl.semaphore_signal(
@@ -165,6 +169,67 @@
             barrier, inc=1, device_id=at(lax.rem(plane + r, planes), spot, grp), device_id_type=MESH
         )
     pl.semaphore_wait(barrier, size + planes - 2)
+
+    def along(up):
+        spot_on_line = plane * up + (planes - 1 - plane) * (1 - up)
+        following = lax.rem(plane + 2 * up - 1 + planes, planes)
+        return 1 - up, spot_on_line, following
+
+    def rows_of(up, s, h):
+        target = (planes - 1 - s) * up + s * (1 - up)
+        return target * chunk + h * rows
+
+    def hop(up, s, h, source):
+        way, _, following = along(up)
+        return pltpu.make_async_remote_copy(
+            src_ref=source,
+            dst_ref=held.at[way, s, h],
+            send_sem=zs.at[way, s, h],
+            recv_sem=zr.at[way, s, h],
+            device_id=at(following, spot, grp),
+            device_id_type=MESH,
+        )
+
+    def begin(s):
+        @pl.when(along(lower)[1] == 0)
+        def _():
+            for h in range(pieces):
+                hop(lower, s, h, part.at[pl.ds(rows_of(lower, s, h), rows)]).start()
+
+    def step(up, s, h):
+        way, here, _ = along(up)
+        end = planes - 1 - s
+
+        @pl.when((here > 0) & (here <= end))
+        def _():
+            hop(up, s, h, held.at[way, s, h]).wait_recv()
+
+        @pl.when((here > 0) & (here < end))
+        def _():
+            start = rows_of(up, s, h)
+
+            def add(i, _):
+                value = held[way, s, h, i].astype(jnp.float32) + part[start + i].astype(jnp.float32)
+                held[way, s, h, i] = value.astype(jnp.bfloat16)
+                return 0
+
+            lax.fori_loop(0, rows, add, 0)
+            hop(up, s, h, held.at[way, s, h]).start()
+
+        @pl.when((here > 0) & (here == end))
+        def _():
+            def add(i, _):
+                total[h * rows + i] += held[way, s, h, i].astype(jnp.float32)
+                return 0
+
+            lax.fori_loop(0, rows, add, 0)
+
+    def finish(up, s, h):
+        way, here, _ = along(up)
+
+        @pl.when(here < planes - 1 - s)
+        def _():
+            hop(up, s, h, held.at[way, s, h]).wait_send()
 
     near = [
         pltpu.make_async_remote_copy(
@@ -179,29 +244,14 @@
     ]
     for copy in near:
         copy.start()
-    mine = pltpu.make_async_copy(part.at[pl.ds(plane * rows, rows)], own, lsem.at[0])
-    mine.start()
-    far = []
-    for r in range(1, planes):
-        target = lax.rem(plane + r, planes)
-        far.append(
-            pltpu.make_async_remote_copy(
-                src_ref=part.at[pl.ds(target * rows, rows)],
-                dst_ref=zin.at[r - 1],
-                send_sem=zs.at[r - 1],
-                recv_sem=zr.at[r - 1],
-                device_id=at(target, spot, grp),
-                device_id_type=MESH,
-            )
-        )
-    for copy in far:
-        copy.start()
-    total = mom[...]
+    begin(0)
+    total[...] = part[pl.ds(plane * chunk, chunk)].astype(jnp.float32)
+    moments = mom[...]
     for copy in near:
         copy.wait()
     for r in range(1, size):
-        total += pin[r - 1]
-    half_sum[...] = total
+        moments += pin[r - 1]
+    half_sum[...] = moments
     wide = [
         pltpu.make_async_remote_copy(
             src_ref=half_sum,
@@ -215,27 +265,27 @@
     ]
     for copy in wide:
         copy.start()
+    for s in range(1, planes - 1):
+        begin(s)
+    for s in range(planes - 1):
+        for up in (lower, 1 - lower):
+            for h in range(pieces):
+                step(up, s, h)
     for copy in wide:
         copy.wait()
-    total = half_sum[...]
+    moments = half_sum[...]
     for r in range(1, planes):
-        total += qin[r - 1]
-    gain = lax.rsqrt(total[:, 0:1] / total[:, 1:2] + 1e-06)
-    gain = jnp.broadcast_to(gain, (angles, width))
-    mine.wait()
-    for copy in far:
-        copy.wait()
+        moments += qin[r - 1]
+    gain = lax.rsqrt(moments[0:1] / moments[1:2] + 1e-06)
+    gain = jnp.broadcast_to(gain, (LANES, LANES)).T[:angles]
 
     def body(i, _):
-        value = own[i].astype(jnp.float32)
-        for r in range(1, planes):
-            value += zin[r - 1, i].astype(jnp.float32)
-        fin[i] = (value * gain).astype(jnp.bfloat16)
+        fin[i] = (total[i] * gain).astype(jnp.bfloat16)
         return 0
 
-    lax.fori_loop(0, rows, body, 0)
-
-    each = rows // size
+    lax.fori_loop(0, chunk, body, 0)
+
+    each = chunk // size
     j, first = share(spot, width, depth)
     view = out.at[:, pl.ds(pl.multiple_of(j * angles, angles), angles), pl.ds(first, width)]
     last = pltpu.make_async_copy(fin.at[pl.ds(spot * each, each)], view, lsem.at[1])
@@ -258,6 +308,10 @@
     last.wait()
     for copy in final:
         copy.wait()
+    for s in range(planes - 1):
+        for up in (lower, 1 - lower):
+            for h in range(pieces):
+                finish(up, s, h)
 
 
 def local(offsets, slant_weights, live, block_tile, image_slot):
@@ -291,7 +345,7 @@
         functools.partial(exchange_kernel, grp),
         out_shape=(
             jax.ShapeDtypeStruct((images, angles, width), jnp.bfloat16),
-            jax.ShapeDtypeStruct((angles, LANES), jnp.float32),
+            jax.ShapeDtypeStruct((8, LANES), jnp.float32),
         ),
         in_specs=[any_space, vmem, vmem],
         out_specs=(vmem, vmem),
@@ -313,21 +367,23 @@
         name="exchange",
     )(offsets.reshape(blocks, 2, hs, depth), aux, slant_weights)
 
-    moments = (angles, LANES)
+    moments = (8, LANES)
+    pieces = 2
+    lines = (2, planes - 1, pieces)
     return pl.pallas_call(
         functools.partial(gather_kernel, grp),
         out_shape=jax.ShapeDtypeStruct((IMG_DEV, 2 * angles, depth), jnp.bfloat16),
-        in_specs=[any_space, vmem],
+        in_specs=[vmem, vmem],
         out_specs=any_space,
         scratch_shapes=[
-            pltpu.VMEM((planes - 1, per_plane, angles, width), jnp.bfloat16),
-            pltpu.VMEM((per_plane, angles, width), jnp.bfloat16),
+            pltpu.VMEM(lines + (per_plane // pieces, angles, width), jnp.bfloat16),
+            pltpu.VMEM((per_plane, angles, width), jnp.float32),
             pltpu.VMEM((per_plane, angles, width), jnp.bfloat16),
             pltpu.VMEM((size - 1,) + moments, jnp.float32),
             pltpu.VMEM((planes - 1,) + moments, jnp.float32),
             pltpu.VMEM(moments, jnp.float32),
-            dma((planes - 1,)),
-            dma((planes - 1,)),
+            dma(lines),
+            dma(lines),
             dma((size - 1,)),
             dma((size - 1,)),
             dma((planes - 1,)),

time: 149 us -> 136 us (0.913)
  Pallas kernels: 142 us -> 129 us
    pallas_call x1, Pallas kernels: 60.9 us -> 48.4 us  [local(): pl.pallas_call(functools.partial(gather_kernel, grp), out_shape=jax.Shape...]
where the time goes in v3:
time: 136 us; the launch traced here: 135 us
  Pallas kernels  129 us (95%)
  local copies, waits for them, and re-layouts  4.06 us (3%)
  other arithmetic  1.86 us (1%)
    pallas_call x1, Pallas kernels, local(): pl.pallas_call(functools.partial(exchange_kernel, grp), out_shape=(jax.Sh...  81 us
    pallas_call x1, Pallas kernels, local(): pl.pallas_call(functools.partial(gather_kernel, grp), out_shape=jax.Shape...  48.4 us
    unnamed x2, local copies, waits for them, and re-layouts  3.26 us

profile of v3, /device:TPU:9, one launch (start us, length us, event | category | flops | bytes accessed | tf_op | source)
XLA Modules:
  0.0 135.4 jit_solution(4279771024115387554)
XLA Ops:
  0.0 0.7 bitcast_add_fusion
  0.7 0.2 select_reduce_fusion.1
  0.9 0.1 select_reduce_fusion
  1.0 0.9 reduce_sum.11
  1.8 1.4 %copy.10.w = bf16[64,32]{1,0:T(8,128)(2,1)} copy(bf16[64,32]{0,1:T(8,128)(2,1)} %param.6) | data formatting | bytes 8192 | tf_op args[1]
  3.2 0.1 reduce_sum.12
  3.4 0.1 copy.9
  3.5 0.6 pad.9.aux
  4.1 81.0 %exchange.1 = (bf16[128,64,128]{2,1,0:T(8,128)(2,1)}, f32[8,128]{1,0:T(8,128)}) custom-call(bf16[96,2,32,512]{3,2,1,0:T(8,128)(2,1)} %bitcast.8, s32[8,128]{1,0:T(8,128)} %pad.9.aux, bf16[64,32]{1,0:T(8,128)(2,1)} %copy.10.w), custom_call_target="tpu_custom_call" | custom-call | tf_op jit(solution)/shard_map/exchange/pallas_call | solution.py:344
  85.1 48.4 %gather.1 = bf16[4,128,512]{2,1,0:T(8,128)(2,1)} custom-call(bf16[128,64,128]{2,1,0:T(8,128)(2,1)} %get-tuple-element.7.part, f32[8,128]{1,0:T(8,128)} %get-tuple-element.8.mom), custom_call_target="tpu_custom_call" | custom-call | tf_op jit(solution)/shard_map/gather/pallas_call | solution.py:373
  133.5 1.9 %copy.12 = bf16[4,128,512]{2,1,0:T(8,128)(2,1)} copy(bf16[4,128,512]{2,1,0:T(8,128)(2,1)} %gather.1) | data formatting | bytes 1048576
  (4 shorter events, 0.0 us)

commit v4 on v3

--- a/solution.py
+++ b/solution.py
@@ -50,17 +50,19 @@
 
 
 def exchange_kernel(
-    grp, off, aux, w, part, mom, raw, aux_in, codes, acc, seg, send, recv, asend, arecv, lsem
+    grp, off, aux, w_in, part, mom, w, raw, aux_in, codes, acc, seg, send, recv, asend, arecv, lsem
 ):
     size = PAIR * grp
     plane, spot = place(grp)
     blocks, depth, width = off.shape[0], off.shape[3], raw.shape[3]
-    angles, images = w.shape[0], acc.shape[0]
+    angles, images = w.shape[1], acc.shape[0]
     j, first = share(spot, width, depth)
     mine = pltpu.make_async_copy(off.at[:, j, :, pl.ds(first, width)], raw.at[0], lsem.at[0])
     mine.start()
     own_codes = pltpu.make_async_copy(aux, codes.at[0], lsem.at[1])
     own_codes.start()
+    weigh = pltpu.make_async_copy(w_in, w, lsem.at[size + 1])
+    weigh.start()
     barrier = pltpu.get_barrier_semaphore()
     for r in range(1, size):
         pl.semaphore_signal(
@@ -96,7 +98,8 @@
     acc[...] = jnp.zeros_like(acc)
     seg[blocks] = jnp.zeros((angles, width), jnp.float32)
     row = lax.broadcasted_iota(jnp.int32, (angles, width), 0)
-    weights = w[...]
+    weigh.wait()
+    weights = w[...].astype(jnp.float32).T.astype(jnp.bfloat16)
     square = jnp.zeros((angles, width), jnp.float32)
     count = jnp.zeros((angles, width), jnp.float32)
     for r in [0] + orders(grp):
@@ -347,9 +350,10 @@
             jax.ShapeDtypeStruct((images, angles, width), jnp.bfloat16),
             jax.ShapeDtypeStruct((8, LANES), jnp.float32),
         ),
-        in_specs=[any_space, vmem, vmem],
+        in_specs=[any_space, vmem, any_space],
         out_specs=(vmem, vmem),
         scratch_shapes=[
+            pltpu.VMEM((hs, angles), jnp.bfloat16),
             pltpu.VMEM((size, blocks, hs, width), jnp.bfloat16),
             pltpu.VMEM((size,) + aux.shape, jnp.int32),
             pltpu.SMEM((size,) + aux.shape, jnp.int32),
@@ -359,16 +363,16 @@
             dma((size - 1,)),
             dma((size - 1,)),
             dma((size - 1,)),
-            dma((size + 1,)),
+            dma((size + 2,)),
         ],
         compiler_params=pltpu.CompilerParams(
             collective_id=0, has_side_effects=True, vmem_limit_bytes=62 * 1024 * 1024
         ),
         name="exchange",
-    )(offsets.reshape(blocks, 2, hs, depth), aux, slant_weights)
+    )(offsets.reshape(blocks, 2, hs, depth), aux, slant_weights.T)
 
     moments = (8, LANES)
-    pieces = 2
+    pieces = 4
     lines = (2, planes - 1, pieces)
     return pl.pallas_call(
         functools.partial(gather_kernel, grp),

time: 136 us -> 134 us (0.985)
  local copies, waits for them, and re-layouts: 4.06 us -> 2.67 us
    unnamed x2 -> x1, local copies, waits for them, and re-layouts: 3.26 us -> 1.87 us
where the time goes in v4:
time: 134 us
  Pallas kernels  130 us (97%)
  local copies, waits for them, and re-layouts  2.67 us (2%)
  other arithmetic  1.86 us (1%)
    pallas_call x1, Pallas kernels, local(): pl.pallas_call(functools.partial(exchange_kernel, grp), out_shape=(jax.Sh...  81 us
    pallas_call x1, Pallas kernels, local(): pl.pallas_call(functools.partial(gather_kernel, grp), out_shape=jax.Shape...  48.6 us

profile of v4, /device:TPU:9, one launch (start us, length us, event | category | flops | bytes accessed | tf_op | source)
XLA Modules:
  0.0 134.2 jit_solution(10829901137267418051)
XLA Ops:
  0.0 0.7 bitcast_add_fusion
  0.7 0.2 select_reduce_fusion.1
  0.9 0.1 select_reduce_fusion
  1.0 0.9 reduce_sum.11
  1.8 0.1 reduce_sum.12
  2.0 0.1 copy.7
  2.1 0.6 pad.9.aux
  2.7 81.0 %exchange.1 = (bf16[128,64,128]{2,1,0:T(8,128)(2,1)}, f32[8,128]{1,0:T(8,128)}) custom-call(bf16[96,2,32,512]{3,2,1,0:T(8,128)(2,1)} %bitcast.9, s32[8,128]{1,0:T(8,128)} %pad.9.aux, bf16[32,64]{1,0:T(8,128)(2,1)} %bitcast.10), custom_call_target="tpu_custom_call" | custom-call | tf_op jit(solution)/shard_map/exchange/pallas_call | solution.py:347
  83.7 48.6 %gather.1 = bf16[4,128,512]{2,1,0:T(8,128)(2,1)} custom-call(bf16[128,64,128]{2,1,0:T(8,128)(2,1)} %get-tuple-element.7.part, f32[8,128]{1,0:T(8,128)} %get-tuple-element.8.mom), custom_call_target="tpu_custom_call" | custom-call | tf_op jit(solution)/shard_map/gather/pallas_call | solution.py:377
  132.3 1.9 %copy.9 = bf16[4,128,512]{2,1,0:T(8,128)(2,1)} copy(bf16[4,128,512]{2,1,0:T(8,128)(2,1)} %gather.1) | data formatting | bytes 1048576
  (4 shorter events, 0.0 us)
